TPU v7x, 32 devices: a whole 2x2x4 slice. The times are simulated.
32 devices in a mesh: dp: 2 (over y), expert: 8 (over z, x), etp: 2 (over core).
Axes of the slice: x: 2, y: 2, z: 4, core: 2. Of those that a mesh axis runs over, the one named last changes fastest.
Arguments:
- tokens: bfloat16 [1024, 4096], P(('dp', 'expert'), 'etp'), may hold values from -6 to 6
- expert_ids: int32 [1024, 8], P(('dp', 'expert')), may hold values from 0 to 15, all different within a row; in each aligned block of 64 rows (0 to 63, 64 to 127, ...) at most 48 rows name the same one
- combine: float32 [1024, 8], P(('dp', 'expert')), may hold values from 0.05 to 1
- gate_weight: bfloat16 [16, 4096, 1536], P('expert', 'dp', 'etp'), may hold values from -0.09375 to 0.09375
- up_weight: bfloat16 [16, 4096, 1536], P('expert', 'dp', 'etp'), may hold values from -0.09375 to 0.09375
- down_weight: bfloat16 [16, 1536, 4096], P('expert', 'etp', 'dp'), may hold values from -0.15625 to 0.15625
Outputs:
- mixed: bfloat16 [1024, 4096], P(('dp', 'expert'), 'etp')
Inputs may be any that keep to these rules, and one draw needn't show every extreme that they name: `expert_ids`: each row names 8 different experts. In the rows of one device (aligned blocks of 64 rows) no expert is named by more than 48 rows, a bound that some block reaches.
All inputs are finite; a program needn't handle non-finite values.
Results may differ from a plain program's by a relative error of at most 0.008.
Values may be sent and summed in bfloat16 or wider, within the bound.
A program may use at most 192 MiB of HBM per device.

v0:
```python
import jax
import jax.numpy as jnp
from jax import lax
from jax.sharding import PartitionSpec as P


def shards(tokens, expert_ids, combine, gate_weight, up_weight, down_weight):
    tok_rows, top_count = expert_ids.shape
    held_count = gate_weight.shape[0]
    groups = lax.axis_size("expert")
    experts = held_count * groups
    capacity = min(tok_rows, 3 * tok_rows * top_count // (2 * experts))
    slots_all = experts * capacity
    onehot = (expert_ids[:, :, None] == jnp.arange(experts, dtype=jnp.int32)[None, None, :]).astype(
        jnp.int32
    )
    flattened = onehot.reshape(tok_rows * top_count, experts)
    before = jnp.cumsum(flattened, axis=0) - flattened
    slot_index = jnp.sum(before * flattened, axis=1).reshape(tok_rows, top_count)
    target = expert_ids * capacity + slot_index
    matches = target[:, :, None] == jnp.arange(slots_all, dtype=jnp.int32)[None, None, :]
    picker = jnp.any(matches, axis=1).astype(jnp.bfloat16)
    weights_map = jnp.sum(jnp.where(matches, combine[:, :, None], 0.0), axis=1)
    gathered = lax.all_gather(tokens, "etp", axis=1, tiled=True)
    packed = jnp.einsum("ts,td->sd", picker, gathered, preferred_element_type=jnp.float32).astype(
        jnp.bfloat16
    )
    arrived = lax.all_to_all(
        packed.reshape(groups, held_count, capacity, gathered.shape[1]),
        "expert",
        split_axis=0,
        concat_axis=2,
        tiled=True,
    )
    inputs = arrived[0]
    gate_part = jnp.einsum(
        "erd,edf->erf",
        inputs,
        lax.all_gather(gate_weight, "dp", axis=1, tiled=True),
        preferred_element_type=jnp.float32,
    )
    up_part = jnp.einsum(
        "erd,edf->erf",
        inputs,
        lax.all_gather(up_weight, "dp", axis=1, tiled=True),
        preferred_element_type=jnp.float32,
    )
    hidden = (jax.nn.silu(gate_part) * up_part).astype(jnp.bfloat16)
    partial_value = jnp.einsum(
        "erf,efd->erd",
        hidden,
        lax.all_gather(down_weight, "dp", axis=2, tiled=True),
        preferred_element_type=jnp.float32,
    ).astype(jnp.bfloat16)
    partial_value = lax.optimization_barrier(partial_value)
    summed = lax.psum_scatter(
        partial_value.astype(jnp.float32).astype(jnp.bfloat16),
        "etp",
        scatter_dimension=2,
        tiled=True,
    )
    returned_rows = lax.all_to_all(summed[None], "expert", split_axis=2, concat_axis=0, tiled=True)
    returned_rows = returned_rows.reshape(slots_all, returned_rows.shape[3])
    weight_high = weights_map.astype(jnp.bfloat16)
    weight_low = (weights_map - weight_high.astype(jnp.float32)).astype(jnp.bfloat16)
    result = jnp.dot(weight_high, returned_rows, preferred_element_type=jnp.float32)
    result = result + jnp.dot(weight_low, returned_rows, preferred_element_type=jnp.float32)
    return result.astype(jnp.bfloat16)


def solution(mesh):
    placed = (
        P(("dp", "expert"), "etp"),
        P(("dp", "expert"), None),
        P(("dp", "expert"), None),
        P("expert", "dp", "etp"),
        P("expert", "dp", "etp"),
        P("expert", "etp", "dp"),
    )
    return jax.shard_map(
        shards, mesh=mesh, in_specs=placed, out_specs=P(("dp", "expert"), "etp"), check_vma=False
    )
```

profile of v0, /device:TPU:0, one launch (start us, length us, event | category | flops | bytes accessed | tf_op | source)
XLA Modules:
  0.0 599.1 jit_solution(10712536201870545837)
XLA Ops:
  6.5 0.7 all-gather.4.cloned.1.call-update
  7.3 0.7 all-gather.6.cloned.1.call-update
  8.0 0.1 copy.46
  8.1 0.1 eq.43
  8.2 0.1 eq.39
  8.3 1.2 reduce-window.6
  9.5 0.2 slice_reduce_fusion
  9.7 0.1 fusion.7
  9.8 0.1 reshape.32
  10.0 0.1 copy.50
  10.1 2.3 all_gather.12
  12.4 0.5 fusion.1
  12.9 4.5 convolution_convert_fusion.1
  17.4 7.8 %all-to-all-start = ((bf16[8,2,48,4096]{3,2,1,0:T(8,128)(2,1)}), bf16[8,2,48,4096]{3,2,1,0:T(8,128)(2,1)}, u32[]{:S(2)}, u32[]{:S(2)}) async-start(bf16[8,2,48,4096]{3,2,1,0:T(8,128)(2,1)} %bitcast.38), calls=%async_computation | async-start | bytes 12582912 | tf_op jit(solution)/shard_map/all_to_all | solution.py:28
  25.3 0.7 all-gather.8.cloned.1.call-update
  26.0 0.2 reduce-scatter.2.cloned.1.call-start
  26.2 137.6 %all-to-all-done = bf16[8,2,48,4096]{3,2,1,0:T(8,128)(2,1)} async-done(((bf16[8,2,48,4096]{3,2,1,0:T(8,128)(2,1)}), bf16[8,2,48,4096]{3,2,1,0:T(8,128)(2,1)}, u32[]{:S(2)}, u32[]{:S(2)}) %all-to-all-start) | async-done | bytes 6291488 | tf_op jit(solution)/shard_map/all_to_all | solution.py:28
  163.8 6.2 %copy.52 = bf16[1,2,8,48,4096]{4,3,2,1,0:T(8,128)(2,1)} copy(bf16[1,2,8,48,4096]{4,3,1,2,0:T(8,128)(2,1)} %bitcast.3) | data formatting | bytes 12582912 | tf_op jit(solution)/shard_map/all_to_all | solution.py:28
  170.0 12.9 %fusion.10 = f32[2,384,768]{2,1,0:T(8,128)S(1)} fusion(bf16[2,384,4096]{2,1,0:T(8,128)(2,1)} %bitcast.42, bf16[2,4096,768]{2,1,0:T(8,128)(2,1)} %all-gather.4.cloned.1.call-done), kind=kOutput, calls=%fused_computation.23 | convolution fusion | flops 4831838208 | bytes 21233664 | tf_op jit(solution)/shard_map/erd,edf->erf/dot_general | solution.py:36
  182.9 133.3 %all-gather.6.cloned.1.call-done = bf16[2,4096,768]{2,1,0:T(8,128)(2,1)} async-done(((bf16[2,2048,768]{2,1,0:T(8,128)(2,1)}), bf16[2,4096,768]{2,1,0:T(8,128)(2,1)}) %all-gather.6.cloned.1.call-update) | async-done | bytes 12582928 | tf_op jit(solution)/shard_map/all_gather | solution.py:45
  316.2 154.1 %all-gather.8.cloned.1.call-done = bf16[2,768,4096]{2,1,0:T(8,128)(2,1)} async-done(((bf16[2,768,2048]{2,1,0:T(8,128)(2,1)}), bf16[2,768,4096]{2,1,0:T(8,128)(2,1)}) %all-gather.8.cloned.1.call-update) | async-done | bytes 12582928 | tf_op jit(solution)/shard_map/all_gather | solution.py:52
  470.3 20.5 %convolution_convert_fusion = bf16[2,384,4096]{2,1,0:T(8,128)(2,1)} fusion(bf16[2,768,4096]{2,1,0:T(8,128)(2,1)} %all-gather.8.cloned.1.call-done, f32[2,384,768]{2,1,0:T(8,128)S(1)} %fusion.10, bf16[2,384,4096]{2,1,0:T(8,128)(2,1)} %bitcast.43, bf16[2,4096,768]{2,1,0:T(8,128)(2,1)} %all-gather.6.cloned.1.call-done), kind=kOutput, calls=%fused_computation | convolution fusion | flops 9670361088 | bytes 40108032 | tf_op jit(solution)/shard_map/erf,efd->erd/dot_general | solution.py:49
  490.9 14.0 %reduce-scatter.2.cloned.1.call-done = bf16[2,384,2048]{2,1,0:T(8,128)(2,1)} async-done(((bf16[2,384,4096]{2,1,0:T(8,128)(2,1)}), bf16[2,384,2048]{2,1,0:T(8,128)(2,1)}) %reduce-scatter.2.cloned.1.call-update) | async-done | bytes 3145744 | tf_op jit(solution)/shard_map/reduce_scatter | solution.py:56
  504.9 6.8 %copy.53 = bf16[1,2,384,2048]{3,1,0,2:T(2,128)(2,1)} copy(bf16[1,2,384,2048]{3,2,1,0:T(8,128)(2,1)} %bitcast.44) | data formatting | bytes 6291456 | tf_op jit(solution)/shard_map/broadcast_in_dim | solution.py:62
  511.7 6.0 %all-to-all-start.1 = ((bf16[1,2,384,2048]{3,1,0,2:T(2,128)(2,1)}), bf16[1,2,384,2048]{3,1,0,2:T(2,128)(2,1)S(1)}, u32[]{:S(2)}, u32[]{:S(2)}) async-start(bf16[1,2,384,2048]{3,1,0,2:T(2,128)(2,1)} %copy.53), calls=%async_computation.2 | async-start | bytes 6291456 | tf_op jit(solution)/shard_map/all_to_all | solution.py:62
  517.8 0.1 copy.51
  517.8 0.5 select_reduce_fusion
  518.4 70.4 %all-to-all-done.1 = bf16[1,2,384,2048]{3,1,0,2:T(2,128)(2,1)S(1)} async-done(((bf16[1,2,384,2048]{3,1,0,2:T(2,128)(2,1)}), bf16[1,2,384,2048]{3,1,0,2:T(2,128)(2,1)S(1)}, u32[]{:S(2)}, u32[]{:S(2)}) %all-to-all-start.1) | async-done | bytes 3145760 | tf_op jit(solution)/shard_map/all_to_all | solution.py:62
  588.8 1.4 copy.54
  590.1 0.4 copy.55
  590.6 0.7 fusion.3
  591.2 1.4 fusion
  (16 shorter events, 0.2 us)
Async XLA Ops:
  6.5 163.5 %all-gather.4.cloned.1.call-start = ((), (), s32[]{:S(2)}) async-start(), calls=%async_computation.3 | async-start | bytes 18874368 | tf_op jit(solution)/shard_map/all_gather | solution.py:39
  7.3 0.8 copy-start.1
  7.3 2.8 copy-start
  7.3 309.0 %all-gather.6.cloned.1.call-start = ((), (), s32[]{:S(2)}) async-start(), calls=%async_computation.4 | async-start | bytes 18874368 | tf_op jit(solution)/shard_map/all_gather | solution.py:45
  17.4 146.3 %all-to-all-start = ((bf16[8,2,48,4096]{3,2,1,0:T(8,128)(2,1)}), bf16[8,2,48,4096]{3,2,1,0:T(8,128)(2,1)}, u32[]{:S(2)}, u32[]{:S(2)}) async-start(bf16[8,2,48,4096]{3,2,1,0:T(8,128)(2,1)} %bitcast.38), calls=%async_computation | async-start | bytes 12582912 | tf_op jit(solution)/shard_map/all_to_all | solution.py:28
  25.3 445.1 %all-gather.8.cloned.1.call-start = ((), (), s32[]{:S(2)}) async-start(), calls=%async_computation.5 | async-start | bytes 18874368 | tf_op jit(solution)/shard_map/all_gather | solution.py:52
  26.0 478.9 %reduce-scatter.2.cloned.1.call-start = ((), (), s32[]{:S(2)}) async-start(), calls=%async_computation.6 | async-start | bytes 9437184 | tf_op jit(solution)/shard_map/reduce_scatter | solution.py:56
  511.7 6.0 %copy-start.2 = (f32[64,8]{0,1:T(8,128)S(1)}, f32[64,8]{0,1:T(8,128)}, u32[]{:S(2)}) copy-start(f32[64,8]{0,1:T(8,128)} %param.8) | copy-start | bytes 6148
  511.7 77.1 %all-to-all-start.1 = ((bf16[1,2,384,2048]{3,1,0,2:T(2,128)(2,1)}), bf16[1,2,384,2048]{3,1,0,2:T(2,128)(2,1)S(1)}, u32[]{:S(2)}, u32[]{:S(2)}) async-start(bf16[1,2,384,2048]{3,1,0,2:T(2,128)(2,1)} %copy.53), calls=%async_computation.2 | async-start | bytes 6291456 | tf_op jit(solution)/shard_map/all_to_all | solution.py:62
Sparse Core Ops, SparseCore 0:
  8.9 154.2 all-gather.3
  164.7 151.4 all-gather.5
  317.8 152.4 all-gather.7
  491.0 13.8 reduce-scatter.1
where the time goes:
time: 600 us; the launch traced here: 599 us
  waiting for transfers between devices  511 us (85%)
  matrix products  40 us (7%)
  local copies, waits for them, and re-layouts  15.7 us (3%)
  starting transfers between devices  14.2 us (2%)
  between operations  13.2 us (2%)
    all_gather x1, waiting for transfers between devices, shards(): lax.all_gather(down_weight, 'dp', axis=2, tiled=True)  154 us
    all_to_all x1, waiting for transfers between devices, shards(): lax.all_to_all(packed.reshape(groups, held_count, capacity, gathered.shap...  138 us
    all_gather x1, waiting for transfers between devices, shards(): lax.all_gather(up_weight, 'dp', axis=1, tiled=True)  133 us
    all_to_all x1, waiting for transfers between devices, shards(): lax.all_to_all(summed[None], 'expert', split_axis=2, concat_axis=0, tiled...  70.4 us
    dot_general x1, matrix products, shards(): jnp.einsum('erf,efd->erd', hidden, lax.all_gather(down_weight, 'dp', axis...  20.5 us
    reduce_scatter x1, waiting for transfers between devices, shards(): lax.psum_scatter(partial_value.astype(jnp.float32).astype(jnp.bfloat16),...  14 us
    dot_general x1, matrix products, shards(): jnp.einsum('erd,edf->erf', inputs, lax.all_gather(gate_weight, 'dp', axis...  12.9 us
  transfers between devices with their start and end apart: 6, of which 5 were waited for; matrix products, arithmetic and copies ran while one was open for 4% of the time, Pallas kernels for 0%

commit v1 on v0

--- a/solution.py
+++ b/solution.py
@@ -39,12 +39,25 @@
         lax.all_gather(gate_weight, "dp", axis=1, tiled=True),
         preferred_element_type=jnp.float32,
     )
-    up_part = jnp.einsum(
+    peers, index = (lax.axis_size("dp"), lax.axis_index("dp"))
+    left = [(i, (i - 1) % peers) for i in range(peers)]
+    rows = up_weight.shape[1]
+    held = up_weight
+    subtotal = jnp.einsum(
         "erd,edf->erf",
-        inputs,
-        lax.all_gather(up_weight, "dp", axis=1, tiled=True),
+        lax.dynamic_slice_in_dim(inputs, index * rows, held.shape[1], axis=2),
+        held,
         preferred_element_type=jnp.float32,
     )
+    for step in range(1, peers):
+        held = lax.ppermute(held, "dp", left)
+        subtotal = subtotal + jnp.einsum(
+            "erd,edf->erf",
+            lax.dynamic_slice_in_dim(inputs, (index + step) % peers * rows, held.shape[1], axis=2),
+            held,
+            preferred_element_type=jnp.float32,
+        )
+    up_part = subtotal
     hidden = (jax.nn.silu(gate_part) * up_part).astype(jnp.bfloat16)
     partial_value = jnp.einsum(
         "erf,efd->erd",

time: 600 us -> 572 us (0.953)
  waiting for transfers between devices: 511 us -> 482 us
    all_gather x1 -> x0, waiting for transfers between devices: 133 us -> none  [shards(): lax.all_gather(up_weight, 'dp', axis=1, tiled=True)]
    all_gather x1, waiting for transfers between devices: 0.01 us -> 125 us  [shards(): lax.all_gather(gate_weight, 'dp', axis=1, tiled=True)]
    all_gather x1, waiting for transfers between devices: 154 us -> 135 us  [shards(): lax.all_gather(down_weight, 'dp', axis=2, tiled=True)]
    dot_general x0 -> x2, matrix products: none -> 11.1 us  [the longest x1 7.08 us: shards(): jnp.einsum('erd,edf->erf', lax.dynamic_slice_in_dim(inputs, (index + step...]
    dot_general x1, matrix products: 20.5 us -> 11.5 us  [shards(): jnp.einsum('erf,efd->erd', hidden, lax.all_gather(down_weight, 'dp', axis...]
  transfers between devices with their start and end apart: 6 -> 6, of which waited for: 5 -> 5; matrix products, arithmetic and copies ran while one was open for 4% -> 6% of each run, Pallas kernels for 0% -> 0%
where the time goes in v1:
time: 572 us; the launch traced here: 571 us
  waiting for transfers between devices  482 us (84%)
  matrix products  40.9 us (7%)
  local copies, waits for them, and re-layouts  15.5 us (3%)
  starting transfers between devices  15.4 us (3%)
  between operations  13.3 us (2%)
    all_to_all x1, waiting for transfers between devices, shards(): lax.all_to_all(packed.reshape(groups, held_count, capacity, gathered.shap...  136 us
    all_gather x1, waiting for transfers between devices, shards(): lax.all_gather(down_weight, 'dp', axis=2, tiled=True)  135 us
    all_gather x1, waiting for transfers between devices, shards(): lax.all_gather(gate_weight, 'dp', axis=1, tiled=True)  125 us
    all_to_all x1, waiting for transfers between devices, shards(): lax.all_to_all(summed[None], 'expert', split_axis=2, concat_axis=0, tiled...  70.4 us
    reduce_scatter x1, waiting for transfers between devices, shards(): lax.psum_scatter(partial_value.astype(jnp.float32).astype(jnp.bfloat16),...  14 us
    dot_general x1, matrix products, shards(): jnp.einsum('erd,edf->erf', inputs, lax.all_gather(gate_weight, 'dp', axis...  11.8 us
    dot_general x1, matrix products, shards(): jnp.einsum('erf,efd->erd', hidden, lax.all_gather(down_weight, 'dp', axis...  11.5 us
  transfers between devices with their start and end apart: 6, of which 5 were waited for; matrix products, arithmetic and copies ran while one was open for 6% of the time, Pallas kernels for 0%

profile of v1, /device:TPU:0, one launch (start us, length us, event | category | flops | bytes accessed | tf_op | source)
XLA Modules:
  0.0 571.4 jit_solution(11469917746390633345)
XLA Ops:
  6.5 0.7 all-gather.3.cloned.1.call-update
  7.4 0.1 eq.45
  7.4 0.1 eq.41
  7.6 1.2 reduce-window.6
  8.7 0.2 slice_reduce_fusion
  9.0 0.1 fusion.13
  9.1 0.1 reshape.32
  9.3 2.3 all_gather.9
  11.6 0.5 fusion.5
  12.2 4.5 convolution_convert_fusion.1
  16.6 7.3 %all-to-all-start = ((bf16[8,2,48,4096]{3,2,1,0:T(8,128)(2,1)}), bf16[8,2,48,4096]{3,2,1,0:T(8,128)(2,1)}, u32[]{:S(2)}, u32[]{:S(2)}) async-start(bf16[8,2,48,4096]{3,2,1,0:T(8,128)(2,1)} %bitcast.39), calls=%async_computation | async-start | bytes 12582912 | tf_op jit(solution)/shard_map/all_to_all | solution.py:28
  24.0 0.7 all-gather.5.cloned.1.call-update
  24.7 0.2 reduce-scatter.2.cloned.1.call-start
  24.9 1.6 collective-permute-start
  26.5 135.9 %all-to-all-done = bf16[8,2,48,4096]{3,2,1,0:T(8,128)(2,1)} async-done(((bf16[8,2,48,4096]{3,2,1,0:T(8,128)(2,1)}), bf16[8,2,48,4096]{3,2,1,0:T(8,128)(2,1)}, u32[]{:S(2)}, u32[]{:S(2)}) %all-to-all-start) | async-done | bytes 6291488 | tf_op jit(solution)/shard_map/all_to_all | solution.py:28
  162.4 3.4 copy.52
  165.8 2.7 copy-done
  168.5 4.0 fusion.2
  172.6 124.9 %all-gather.3.cloned.1.call-done = bf16[2,4096,768]{2,1,0:T(8,128)(2,1)} async-done(((bf16[2,2048,768]{2,1,0:T(8,128)(2,1)}), bf16[2,4096,768]{2,1,0:T(8,128)(2,1)}) %all-gather.3.cloned.1.call-update) | async-done | bytes 12582928 | tf_op jit(solution)/shard_map/all_gather | solution.py:39
  297.5 11.8 %fusion.17 = f32[2,384,768]{2,1,0:T(8,128)S(1)} fusion(bf16[2,384,4096]{2,1,0:T(8,128)(2,1)} %bitcast.44, bf16[2,4096,768]{2,1,0:T(8,128)(2,1)} %all-gather.3.cloned.1.call-done), kind=kOutput, calls=%fused_computation.28 | convolution fusion | flops 4831838208 | bytes 21233664 | tf_op jit(solution)/shard_map/erd,edf->erf/dot_general | solution.py:36
  309.4 7.1 %multiply_convert_fusion = bf16[2,384,768]{2,1,0:T(8,128)(2,1)S(1)} fusion(f32[2,384,768]{2,1,0:T(8,128)S(1)} %copy-done.5, f32[2,384,768]{2,1,0:T(8,128)S(1)} %fusion.17, bf16[2,2048,768]{2,1,0:T(8,128)(2,1)} %collective-permute-done, bf16[2,384,4096]{2,1,0:T(8,128)(2,1)S(1)} %bitcast.45, s32[]{:T(128)S(6)} %select_n.20), kind=kOutput, calls=%fused_computation.6 | convolution fusion | flops 2420047872 | bytes 15335428 | tf_op jit(solution)/shard_map/erd,edf->erf/dot_general | solution.py:54
  316.4 135.1 %all-gather.5.cloned.1.call-done = bf16[2,768,4096]{2,1,0:T(8,128)(2,1)} async-done(((bf16[2,768,2048]{2,1,0:T(8,128)(2,1)}), bf16[2,768,4096]{2,1,0:T(8,128)(2,1)}) %all-gather.5.cloned.1.call-update) | async-done | bytes 12582928 | tf_op jit(solution)/shard_map/all_gather | solution.py:65
  451.5 11.5 %convolution_convert_fusion = bf16[2,384,4096]{2,1,0:T(8,128)(2,1)} fusion(bf16[2,384,768]{2,1,0:T(8,128)(2,1)S(1)} %multiply_convert_fusion, bf16[2,768,4096]{2,1,0:T(8,128)(2,1)} %all-gather.5.cloned.1.call-done), kind=kOutput, calls=%fused_computation | convolution fusion | flops 4834983936 | bytes 20054016 | tf_op jit(solution)/shard_map/erf,efd->erd/dot_general | solution.py:62
  463.0 14.0 %reduce-scatter.2.cloned.1.call-done = bf16[2,384,2048]{2,1,0:T(8,128)(2,1)} async-done(((bf16[2,384,4096]{2,1,0:T(8,128)(2,1)}), bf16[2,384,2048]{2,1,0:T(8,128)(2,1)}) %reduce-scatter.2.cloned.1.call-update) | async-done | bytes 3145744 | tf_op jit(solution)/shard_map/reduce_scatter | solution.py:69
  477.0 6.8 %copy.53 = bf16[1,2,384,2048]{3,1,0,2:T(2,128)(2,1)} copy(bf16[1,2,384,2048]{3,2,1,0:T(8,128)(2,1)} %bitcast.46) | data formatting | bytes 6291456 | tf_op jit(solution)/shard_map/broadcast_in_dim | solution.py:75
  483.8 6.3 %all-to-all-start.1 = ((bf16[1,2,384,2048]{3,1,0,2:T(2,128)(2,1)}), bf16[1,2,384,2048]{3,1,0,2:T(2,128)(2,1)S(1)}, u32[]{:S(2)}, u32[]{:S(2)}) async-start(bf16[1,2,384,2048]{3,1,0,2:T(2,128)(2,1)} %copy.53), calls=%async_computation.2 | async-start | bytes 6291456 | tf_op jit(solution)/shard_map/all_to_all | solution.py:75
  490.2 0.5 select_reduce_fusion
  490.7 70.4 %all-to-all-done.1 = bf16[1,2,384,2048]{3,1,0,2:T(2,128)(2,1)S(1)} async-done(((bf16[1,2,384,2048]{3,1,0,2:T(2,128)(2,1)}), bf16[1,2,384,2048]{3,1,0,2:T(2,128)(2,1)S(1)}, u32[]{:S(2)}, u32[]{:S(2)}) %all-to-all-start.1) | async-done | bytes 3145760 | tf_op jit(solution)/shard_map/all_to_all | solution.py:75
  561.1 1.4 copy.54
  562.5 0.4 copy.55
  562.9 0.7 fusion.9
  563.5 1.4 fusion.4
  (28 shorter events, 0.5 us)
Async XLA Ops:
  6.5 0.7 copy-start.3
  6.5 2.8 copy-start.2
  6.5 290.9 %all-gather.3.cloned.1.call-start = ((), (), s32[]{:S(2)}) async-start(), calls=%async_computation.3 | async-start | bytes 18874368 | tf_op jit(solution)/shard_map/all_gather | solution.py:39
  16.6 145.8 %all-to-all-start = ((bf16[8,2,48,4096]{3,2,1,0:T(8,128)(2,1)}), bf16[8,2,48,4096]{3,2,1,0:T(8,128)(2,1)}, u32[]{:S(2)}, u32[]{:S(2)}) async-start(bf16[8,2,48,4096]{3,2,1,0:T(8,128)(2,1)} %bitcast.39), calls=%async_computation | async-start | bytes 12582912 | tf_op jit(solution)/shard_map/all_to_all | solution.py:28
  23.9 427.6 %all-gather.5.cloned.1.call-start = ((), (), s32[]{:S(2)}) async-start(), calls=%async_computation.4 | async-start | bytes 18874368 | tf_op jit(solution)/shard_map/all_gather | solution.py:65
  24.0 144.5 %slice-start = ((s8[6291456]{0:T(1024)(128)(4,1)}), s8[2097152]{0:T(1024)(128)(4,1)S(1)}, s32[]{:S(2)}) async-start(s8[6291456]{0:T(1024)(128)(4,1)} %bitcast.47), calls=%async_computation.6 | async-start | bytes 4194304
  24.7 452.4 %reduce-scatter.2.cloned.1.call-start = ((), (), s32[]{:S(2)}) async-start(), calls=%async_computation.5 | async-start | bytes 9437184 | tf_op jit(solution)/shard_map/reduce_scatter | solution.py:69
  24.9 284.4 %collective-permute-start = (bf16[2,2048,768]{2,1,0:T(8,128)(2,1)}, bf16[2,2048,768]{2,1,0:T(8,128)(2,1)}, u32[]{:S(2)}, u32[]{:S(2)}) collective-permute-start(bf16[2,2048,768]{2,1,0:T(8,128)(2,1)} %param.10), channel_id=1, source_target_pairs={{0,16},{16,0},{1,17},{17,1},{2,18},{18,2},{3,19},{19,3},{4,20},{20... | collective-permute-start | bytes 18874376 | tf_op jit(solution)/shard_map/ppermute | solution.py:53
  162.4 6.1 %slice-start.1 = ((s8[6291456]{0:T(1024)(128)(4,1)}), s8[4194304]{0:T(1024)(128)(4,1)S(1)}, s32[]{:S(2)}) async-start(s8[6291456]{0:T(1024)(128)(4,1)} %bitcast.47), calls=%async_computation.7 | async-start | bytes 8388608
  165.8 2.7 copy-start
  297.5 11.9 %copy-start.1 = (bf16[1,2,8,48,4096]{4,3,2,1,0:T(8,128)(2,1)S(1)}, bf16[1,2,8,48,4096]{4,3,2,1,0:T(8,128)(2,1)}, u32[]{:S(2)}) copy-start(bf16[1,2,8,48,4096]{4,3,2,1,0:T(8,128)(2,1)} %copy-done) | copy-start | bytes 18874372
  297.5 11.9 %copy-start.5 = (f32[2,384,768]{2,1,0:T(8,128)S(1)}, f32[2,384,768]{2,1,0:T(8,128)}, u32[]{:S(2)}) copy-start(f32[2,384,768]{2,1,0:T(8,128)} %fusion.2) | copy-start | bytes 7077892
  483.8 6.3 %copy-start.4 = (f32[64,8]{0,1:T(8,128)S(1)}, f32[64,8]{0,1:T(8,128)}, u32[]{:S(2)}) copy-start(f32[64,8]{0,1:T(8,128)} %param.8) | copy-start | bytes 6148
  483.8 77.3 %all-to-all-start.1 = ((bf16[1,2,384,2048]{3,1,0,2:T(2,128)(2,1)}), bf16[1,2,384,2048]{3,1,0,2:T(2,128)(2,1)S(1)}, u32[]{:S(2)}, u32[]{:S(2)}) async-start(bf16[1,2,384,2048]{3,1,0,2:T(2,128)(2,1)} %copy.53), calls=%async_computation.2 | async-start | bytes 6291456 | tf_op jit(solution)/shard_map/all_to_all | solution.py:75
Sparse Core Ops, SparseCore 0:
  8.9 288.5 all-gather.2
  299.0 152.4 all-gather.4
  463.2 13.8 reduce-scatter.1
